TPU v7x, 8 devices: a whole 2x2x1 slice. The times are simulated.
8 devices in a mesh: dp: 2 (over z, y), ep: 4 (over x, core).
Axes of the slice: x: 2, y: 2, z: 1, core: 2. Of those that a mesh axis runs over, the one named last changes fastest.
Arguments:
- tok_x: bfloat16 [8192, 4096], P(('dp', 'ep'))
- tok_dy: bfloat16 [8192, 4096], P(('dp', 'ep'))
- exp_first: int32 [8192], P(('dp', 'ep'))
- exp_second: int32 [8192], P(('dp', 'ep'))
- eligible: int32 [8192, 8], P(('dp', 'ep'))
- slot_first: int32 [8192], P(('dp', 'ep'))
- slot_second: int32 [8192], P(('dp', 'ep'))
- ln_weight: bfloat16 [4096], replicated
- ln_bias: bfloat16 [4096], replicated
- router: bfloat16 [4096, 8], replicated
- w_gate: bfloat16 [8, 4096, 1376], P('ep')
- w_up: bfloat16 [8, 4096, 1376], P('ep')
- w_down: bfloat16 [8, 1376, 4096], P('ep')
Outputs:
- output 1: bfloat16 [8192, 4096], P(('dp', 'ep'))
- output 2: bfloat16 [8192, 4096], P(('dp', 'ep'))
- output 3: float32 [8, 4096, 1376], P('ep')
- output 4: float32 [8, 4096, 1376], P('ep')
- output 5: float32 [8, 1376, 4096], P('ep')
- output 6: float32 [4096, 8], replicated
- output 7: float32 [4096], replicated
- output 8: float32 [4096], replicated
All inputs are finite; a program needn't handle non-finite values.
Results may differ from a plain program's by a relative error of at most 0.00492321.
Values are sent between devices in bfloat16 or wider.
A program may use at most 1 GiB of HBM per device.

v0:
```python
import jax
import jax.numpy as jnp
from jax import lax
from jax.sharding import PartitionSpec as P

LN_EPS = 1e-5


def layer_norm(x_rows, ln_weight, ln_bias):
    x_float = x_rows.astype(jnp.float32)
    centered = x_float - jnp.mean(x_float, axis=-1, keepdims=True)
    inv_std = lax.rsqrt(jnp.mean(centered * centered, axis=-1, keepdims=True) + LN_EPS)
    x_hat = centered * inv_std
    hidden = (x_hat * ln_weight.astype(jnp.float32) + ln_bias.astype(jnp.float32)).astype(jnp.bfloat16)
    return hidden, x_hat, inv_std


def layer_norm_back(grad_h, x_hat, inv_std, ln_weight):
    scaled = grad_h * ln_weight.astype(jnp.float32)
    return inv_std * (scaled - jnp.mean(scaled, axis=-1, keepdims=True)
                      - x_hat * jnp.mean(scaled * x_hat, axis=-1, keepdims=True))


def masked_gate(logits, allowed, choice):
    expert_ids = jnp.arange(logits.shape[-1])
    prob_all = jax.nn.softmax(jnp.where(allowed, logits, -1e30), axis=-1)
    picked = (choice[:, None] == expert_ids[None, :]).astype(jnp.float32)
    return jnp.sum(prob_all * picked, axis=-1), prob_all, picked


def solution(mesh):
    n_ep = mesh.shape['ep']
    tok_spec = P(('dp', 'ep'), None)
    row_spec = P(('dp', 'ep'))
    exp_spec = P('ep', None, None)

    def local_step(tok_x, tok_dy, exp_first, exp_second, eligible, slot_first, slot_second,
                   ln_weight, ln_bias, router, w_gate, w_up, w_down):
        n_local, d_model = tok_x.shape
        n_exp = eligible.shape[1]
        local_exp = w_gate.shape[0]
        slot_cap = 3 * n_local // n_exp
        f32 = jnp.float32
        hidden, x_hat, inv_std = layer_norm(tok_x, ln_weight, ln_bias)
        logits = jnp.dot(hidden, router, preferred_element_type=f32)
        expert_ids = jnp.arange(n_exp)
        allowed = eligible > 0
        gate_one, prob_one, pick_one = masked_gate(logits, allowed, exp_first)
        gate_two, prob_two, pick_two = masked_gate(logits, allowed & (expert_ids[None, :] != exp_first[:, None]), exp_second)
        row_ids = jnp.arange(n_exp * slot_cap)
        pos_one = jnp.where(slot_first >= 0, exp_first * slot_cap + slot_first, -1)
        pos_two = jnp.where(slot_second >= 0, exp_second * slot_cap + slot_second, -1)
        sel_one = (pos_one[:, None] == row_ids[None, :]).astype(jnp.bfloat16)
        sel_two = (pos_two[:, None] == row_ids[None, :]).astype(jnp.bfloat16)
        sel_both = sel_one + sel_two
        hid_buf = jnp.einsum('tp,td->pd', sel_both, hidden, preferred_element_type=f32).astype(jnp.bfloat16)
        hid_recv = lax.all_to_all(hid_buf.reshape(n_ep, local_exp, slot_cap, d_model), 'ep', 0, 0, tiled=True)
        pre_gate = jnp.einsum('sgcd,gdf->sgcf', hid_recv, w_gate, preferred_element_type=f32)
        pre_up = jnp.einsum('sgcd,gdf->sgcf', hid_recv, w_up, preferred_element_type=f32)
        sig_gate = jax.nn.sigmoid(pre_gate)
        silu_gate = pre_gate * sig_gate
        inner_act = (silu_gate * pre_up).astype(jnp.bfloat16)
        exp_out = jnp.einsum('sgcf,gfd->sgcd', inner_act, w_down, preferred_element_type=f32).astype(jnp.bfloat16)
        out_back = lax.all_to_all(exp_out, 'ep', 0, 0, tiled=True).reshape(n_exp * slot_cap, d_model)
        out_one = jnp.dot(sel_one, out_back, preferred_element_type=f32)
        out_two = jnp.dot(sel_two, out_back, preferred_element_type=f32)
        y_mix = gate_one[:, None] * out_one + gate_two[:, None] * out_two
        out_tok = (tok_x.astype(f32) + y_mix).astype(jnp.bfloat16)
        dy_float = tok_dy.astype(f32)
        grad_one = (gate_one[:, None] * dy_float).astype(jnp.bfloat16)
        grad_two = (gate_two[:, None] * dy_float).astype(jnp.bfloat16)
        grad_buf = (jnp.einsum('tp,td->pd', sel_one, grad_one, preferred_element_type=f32)
                    + jnp.einsum('tp,td->pd', sel_two, grad_two, preferred_element_type=f32)).astype(jnp.bfloat16)
        grad_recv = lax.all_to_all(grad_buf.reshape(n_ep, local_exp, slot_cap, d_model), 'ep', 0, 0, tiled=True)
        grad_inner = jnp.einsum('sgcd,gfd->sgcf', grad_recv, w_down, preferred_element_type=f32)
        dw_down = jnp.einsum('sgcf,sgcd->gfd', inner_act, grad_recv, preferred_element_type=f32)
        grad_pre_gate = (grad_inner * pre_up * sig_gate * (1.0 + pre_gate * (1.0 - sig_gate))).astype(jnp.bfloat16)
        grad_pre_up = (grad_inner * silu_gate).astype(jnp.bfloat16)
        dw_gate = jnp.einsum('sgcd,sgcf->gdf', hid_recv, grad_pre_gate, preferred_element_type=f32)
        dw_up = jnp.einsum('sgcd,sgcf->gdf', hid_recv, grad_pre_up, preferred_element_type=f32)
        grad_hid = (jnp.einsum('sgcf,gdf->sgcd', grad_pre_gate, w_gate, preferred_element_type=f32)
                    + jnp.einsum('sgcf,gdf->sgcd', grad_pre_up, w_up, preferred_element_type=f32)).astype(jnp.bfloat16)
        hid_back = lax.all_to_all(grad_hid, 'ep', 0, 0, tiled=True).reshape(n_exp * slot_cap, d_model)
        grad_exp = jnp.dot(sel_both, hid_back, preferred_element_type=f32)
        dgate_one = jnp.sum(dy_float * out_one, axis=-1)
        dgate_two = jnp.sum(dy_float * out_two, axis=-1)
        d_logits = ((dgate_one * gate_one)[:, None] * (pick_one - prob_one)
                    + (dgate_two * gate_two)[:, None] * (pick_two - prob_two)).astype(jnp.bfloat16)
        d_router = jnp.einsum('td,te->de', hidden, d_logits, preferred_element_type=f32)
        grad_h = jnp.einsum('te,de->td', d_logits, router, preferred_element_type=f32) + grad_exp
        d_ln_weight = jnp.sum(grad_h * x_hat, axis=0)
        d_ln_bias = jnp.sum(grad_h, axis=0)
        dx_tok = (dy_float + layer_norm_back(grad_h, x_hat, inv_std, ln_weight)).astype(jnp.bfloat16)
        dw_gate = lax.psum(dw_gate, 'dp')
        dw_up = lax.psum(dw_up, 'dp')
        dw_down = lax.psum(dw_down, 'dp')
        d_router = lax.psum(d_router, ('dp', 'ep'))
        d_ln_weight = lax.psum(d_ln_weight, ('dp', 'ep'))
        d_ln_bias = lax.psum(d_ln_bias, ('dp', 'ep'))
        return out_tok, dx_tok, dw_gate, dw_up, dw_down, d_router, d_ln_weight, d_ln_bias

    return jax.shard_map(
        local_step, mesh=mesh,
        in_specs=(tok_spec, tok_spec, row_spec, row_spec, tok_spec, row_spec, row_spec,
                  P(), P(), P(), exp_spec, exp_spec, exp_spec),
        out_specs=(tok_spec, tok_spec, exp_spec, exp_spec, exp_spec, P(), P(), P()),
        check_vma=False)
```

profile of v0, /device:TPU:0, one launch (start us, length us, event | category | flops | bytes accessed | tf_op | source)
XLA Modules:
  0.0 4181.1 jit_solution(2308036031251749598)
XLA Ops:
  24.4 33.4 convolution_convert_fusion
  72.9 33.9 fusion.51
  106.8 38.5 add_convert_fusion.1
  145.3 194.7 %all-to-all-done = bf16[4,2,384,4096]{3,2,1,0:T(8,128)(2,1)} async-done(((bf16[4,2,384,4096]{3,2,1,0:T(8,128)(2,1)}), bf16[4,2,384,4096]{3,2,1,0:T(8,128)(2,1)}, u32[]{:S(2)}, u32[]{:S(2)}) %all-to-all-start) | async-done | bytes 25165856 | tf_op jit(solution)/shard_map/all_to_all | solution.py:57
  348.4 44.6 %fusion.3 = f32[2,4,384,1376]{2,3,1,0:T(8,128)} fusion(bf16[2,4096,1376]{1,2,0:T(8,128)(2,1)} %param.24, bf16[4,2,384,4096]{3,2,1,0:T(8,128)(2,1)} %all-to-all-done), kind=kOutput, calls=%fused_computation.18 | convolution fusion | flops 34628173824 | bytes 64618496 | tf_op jit(solution)/shard_map/sgcd,gdf->sgcf/dot_general | solution.py:59
  393.0 44.2 %fusion.7 = f32[2,4,384,1376]{2,3,1,0:T(8,128)} fusion(bf16[2,4096,1376]{1,2,0:T(8,128)(2,1)} %param.23, bf16[4,2,384,4096]{3,2,1,0:T(8,128)(2,1)} %all-to-all-done), kind=kOutput, calls=%fused_computation.22 | convolution fusion | flops 34628173824 | bytes 64618496 | tf_op jit(solution)/shard_map/sgcd,gdf->sgcf/dot_general | solution.py:58
  437.2 183.8 %all-to-all-done.2 = bf16[4,2,384,4096]{3,2,1,0:T(8,128)(2,1)} async-done(((bf16[4,2,384,4096]{3,2,1,0:T(8,128)(2,1)}), bf16[4,2,384,4096]{3,2,1,0:T(8,128)(2,1)}, u32[]{:S(2)}, u32[]{:S(2)}) %all-to-all-start.2) | async-done | bytes 25165856 | tf_op jit(solution)/shard_map/all_to_all | solution.py:74
  621.0 64.4 %fusion.25 = (bf16[4,2,384,1376]{2,3,0,1:T(8,128)(2,1)}, bf16[4,2,384,1376]{2,3,0,1:T(8,128)(2,1)}, bf16[4,2,384,1376]{2,3,0,1:T(8,128)(2,1)}) fusion(f32[2,4,384,1376]{2,3,1,0:T(8,128)} %fusion.3, f32[2,4,384,1376]{2,3,1,0:T(8,128)} %fusion.7, bf16[2,1376,4096]{2,1,0:T(8,128)(2,1)} %param.25, bf16[4,2,384,4096]{3,2,1,0:T(8,128)(2,1)} %all-to-all-done.2), kind=kOutput, calls=%fused_computation.42 | convolution fusion | flops 34691579904 | bytes 106889216 | tf_op jit(solution)/shard_map/sgcd,gfd->sgcf/dot_general | solution.py:75
  685.4 47.0 %convert_bitcast_fusion = bf16[4,2,384,4096]{3,2,0,1:T(8,128)(2,1)} fusion(bf16[4,2,384,1376]{2,3,0,1:T(8,128)(2,1)} %get-tuple-element.25, bf16[2,1376,4096]{2,1,0:T(8,128)(2,1)} %param.25), kind=kOutput, calls=%fused_computation.11 | convolution fusion | flops 34640756736 | bytes 56164352 | tf_op jit(solution)/shard_map/sgcf,gfd->sgcd/dot_general | solution.py:63
  744.6 278.3 %all_to_all.20 = bf16[4,2,384,4096]{3,2,1,0:T(8,128)(2,1)} all-to-all(bf16[4,2,384,4096]{3,2,1,0:T(8,128)(2,1)S(1)} %copy.29), channel_id=1, replica_groups=mesh['dp'=2,'ep'=4] {'ep'}, dimensions={0} | all-to-all | bytes 50331648 | tf_op jit(solution)/shard_map/all_to_all | solution.py:64
  1023.0 31.6 fusion.49
  1054.7 36.4 fusion.40
  1097.7 44.5 %convolution_bitcast_fusion.2 = f32[2,1376,4096]{2,1,0:T(8,128)} fusion(bf16[4,2,384,1376]{2,3,0,1:T(8,128)(2,1)} %get-tuple-element.25, bf16[4,2,384,4096]{3,2,1,0:T(8,128)(2,1)} %all-to-all-done.2), kind=kOutput, calls=%fused_computation.9 | convolution fusion | flops 34628173824 | bytes 78708736 | tf_op jit(solution)/shard_map/sgcf,sgcd->gfd/dot_general | solution.py:76
  1142.3 44.6 %convolution_bitcast_fusion.1 = f32[2,4096,1376]{1,2,0:T(8,128)} fusion(bf16[4,2,384,4096]{3,2,1,0:T(8,128)(2,1)} %all-to-all-done, bf16[4,2,384,1376]{2,3,0,1:T(8,128)(2,1)} %get-tuple-element.24), kind=kOutput, calls=%fused_computation.8 | convolution fusion | flops 34628173824 | bytes 78708736 | tf_op jit(solution)/shard_map/sgcd,sgcf->gdf/dot_general | solution.py:79
  1186.8 44.7 %convolution_bitcast_fusion = f32[2,4096,1376]{1,2,0:T(8,128)} fusion(bf16[4,2,384,4096]{3,2,1,0:T(8,128)(2,1)} %all-to-all-done, bf16[4,2,384,1376]{2,3,0,1:T(8,128)(2,1)} %get-tuple-element.26), kind=kOutput, calls=%fused_computation.7 | convolution fusion | flops 34628173824 | bytes 78708736 | tf_op jit(solution)/shard_map/sgcd,sgcf->gdf/dot_general | solution.py:80
  1231.6 48.7 %fusion.1 = f32[2,4,384,4096]{3,2,1,0:T(8,128)} fusion(bf16[4,2,384,1376]{2,3,0,1:T(8,128)(2,1)} %get-tuple-element.26, bf16[2,4096,1376]{1,2,0:T(8,128)(2,1)} %param.24), kind=kOutput, calls=%fused_computation.16 | convolution fusion | flops 34628173824 | bytes 81330176 | tf_op jit(solution)/shard_map/sgcf,gdf->sgcd/dot_general | solution.py:82
  1280.3 53.1 %fusion = bf16[4,2,384,4096]{3,2,0,1:T(8,128)(2,1)} fusion(f32[2,4,384,4096]{3,2,1,0:T(8,128)} %fusion.1, bf16[4,2,384,1376]{2,3,0,1:T(8,128)(2,1)} %get-tuple-element.24, bf16[2,4096,1376]{1,2,0:T(8,128)(2,1)} %param.23), kind=kOutput, calls=%fused_computation.10 | convolution fusion | flops 34653339648 | bytes 106496000 | tf_op jit(solution)/shard_map/sgcf,gdf->sgcd/dot_general | solution.py:81
  1345.6 278.3 %all_to_all.21 = bf16[4,2,384,4096]{3,2,1,0:T(8,128)(2,1)} all-to-all(bf16[4,2,384,4096]{3,2,1,0:T(8,128)(2,1)S(1)} %copy.31), channel_id=1, replica_groups=mesh['dp'=2,'ep'=4] {'ep'}, dimensions={0} | all-to-all | bytes 50331648 | tf_op jit(solution)/shard_map/all_to_all | solution.py:83
  1624.1 31.7 fusion.61
  1711.9 412.4 %all-reduce.6.cloned.1.call-done = f32[2,1376,4096]{2,1,0:T(8,128)} async-done(((f32[2,1376,4096]{2,1,0:T(8,128)}), f32[2,1376,4096]{2,1,0:T(8,128)}) %all-reduce.6.cloned.1.call-update) | async-done | bytes 45088784 | tf_op jit(solution)/shard_map/psum | solution.py:96
  2124.3 1954.0 %all-reduce.10.cloned.1.call-done = (f32[2,4096,1376]{1,2,0:T(8,128)}, f32[2,4096,1376]{1,2,0:T(8,128)}) async-done(((f32[2,4096,1376]{1,2,0:T(8,128)}, f32[2,4096,1376]{1,2,0:T(8,128)}), (f32[2,4096,1376]{1,2,0:T(8,128)}, f32[2,4096,1376]{1,2,0:T(8,128)})) %all-reduce.10.cloned.1.call-update) | async-done | bytes 90177552 | tf_op jit(solution)/shard_map/psum | solution.py:94
  4078.3 31.7 copy.61
  4110.0 31.7 copy.62
  4141.7 31.8 copy.63
  (142 shorter events, 128.3 us)
Async XLA Ops:
  7.2 59.3 %copy-start = (bf16[4096,8]{0,1:T(8,128)(2,1)S(1)}, bf16[4096,8]{0,1:T(8,128)(2,1)}, u32[]{:S(2)}) copy-start(bf16[4096,8]{0,1:T(8,128)(2,1)} %param.22) | copy-start | bytes 196612
  13.9 43.8 %copy-start.20 = (f32[1024]{0:T(1024)}, f32[1024]{0:T(1024)S(1)}, u32[]{:S(2)}) copy-start(f32[1024]{0:T(1024)S(1)} %broadcast_multiply_fusion.2) | copy-start | bytes 12292
  19.7 38.1 copy-start.32
  24.3 48.5 %copy-start.47 = (s32[1024]{0:T(1024)}, s32[1024]{0:T(1024)S(1)}, u32[]{:S(2)}) copy-start(s32[1024]{0:T(1024)S(1)} %get-tuple-element.31) | copy-start | bytes 12292
  24.4 82.4 %copy-start.44 = (s32[1024]{0:T(1024)}, s32[1024]{0:T(1024)S(1)}, u32[]{:S(2)}) copy-start(s32[1024]{0:T(1024)S(1)} %get-tuple-element.30) | copy-start | bytes 12292
  57.7 282.2 %all-to-all-start = ((bf16[4,2,384,4096]{3,2,1,0:T(8,128)(2,1)}), bf16[4,2,384,4096]{3,2,1,0:T(8,128)(2,1)}, u32[]{:S(2)}, u32[]{:S(2)}) async-start(bf16[4,2,384,4096]{3,2,1,0:T(8,128)(2,1)} %bitcast.98), calls=%async_computation | async-start | bytes 50331648 | tf_op jit(solution)/shard_map/all_to_all | solution.py:57
  72.3 34.5 copy-start.38
  72.9 33.9 copy-start.40
  340.0 281.0 %all-to-all-start.2 = ((bf16[4,2,384,4096]{3,2,1,0:T(8,128)(2,1)}), bf16[4,2,384,4096]{3,2,1,0:T(8,128)(2,1)}, u32[]{:S(2)}, u32[]{:S(2)}) async-start(bf16[4,2,384,4096]{3,2,1,0:T(8,128)(2,1)} %bitcast.99), calls=%async_computation.2 | async-start | bytes 50331648 | tf_op jit(solution)/shard_map/all_to_all | solution.py:74
  348.4 1363.5 %all-reduce.8.cloned.1.call-start = ((), (), s32[]{:S(2)}) async-start(), calls=%async_computation.5 | async-start | bytes 262144 | tf_op jit(solution)/shard_map/psum | solution.py:97
  744.6 278.4 %copy-start.45 = (s32[1024]{0:T(1024)S(1)}, s32[1024]{0:T(1024)}, u32[]{:S(2)}) copy-start(s32[1024]{0:T(1024)} %copy-done.44) | copy-start | bytes 12292
  1054.6 37.7 copy-start.3
  1054.6 37.7 copy-start.6
  1054.7 37.7 copy-start.12
  1054.7 37.7 copy-start.15
  1054.7 37.7 copy-start.18
  1054.7 37.7 copy-start.24
  1054.7 37.7 copy-start.27
  1054.7 37.7 copy-start.30
  1097.6 1026.6 %all-reduce.6.cloned.1.call-start = ((), (), s32[]{:S(2)}) async-start(), calls=%async_computation.4 | async-start | bytes 90177536 | tf_op jit(solution)/shard_map/psum | solution.py:96
  1142.2 2936.1 %all-reduce.10.cloned.1.call-start = ((), (), s32[]{:S(2)}) async-start(), calls=%async_computation.6 | async-start | bytes 180355072 | tf_op jit(solution)/shard_map/psum | solution.py:94
  1345.6 278.4 %copy-start.46 = (s32[1024]{0:T(1024)S(1)}, s32[1024]{0:T(1024)}, u32[]{:S(2)}) copy-start(s32[1024]{0:T(1024)} %copy-done.44) | copy-start | bytes 12292
  1345.6 278.4 %copy-start.49 = (s32[1024]{0:T(1024)S(1)}, s32[1024]{0:T(1024)}, u32[]{:S(2)}) copy-start(s32[1024]{0:T(1024)} %copy-done.47) | copy-start | bytes 12292
  1345.6 310.2 %slice-start.2 = ((s8[8388608]{0:T(1024)(128)(4,1)}), s8[4194304]{0:T(1024)(128)(4,1)S(1)}, s32[]{:S(2)}) async-start(s8[8388608]{0:T(1024)(128)(4,1)} %bitcast.96), calls=%async_computation.9 | async-start | bytes 8388608
  (35 other events, 718.0 us)
Sparse Core Ops, SparseCore 0:
  1097.8 43.0 all-reduce.7
  1143.9 980.3 all-reduce.5
  2127.3 1950.8 all-reduce.9
where the time goes:
time: 4190 us; the launch traced here: 4180 us
  waiting for transfers between devices  2740 us (65%)
  matrix products  667 us (16%)
  blocking collectives  581 us (14%)
  local copies, waits for them, and re-layouts  122 us (3%)
    psum x1, waiting for transfers between devices, local_step(): dw_gate = lax.psum(dw_gate, 'dp')  1950 us
    psum x1, waiting for transfers between devices, local_step(): dw_down = lax.psum(dw_down, 'dp')  412 us
    all_to_all x1, blocking collectives, local_step(): lax.all_to_all(exp_out, 'ep', 0, 0, tiled=True)  278 us
    all_to_all x1, blocking collectives, local_step(): lax.all_to_all(grad_hid, 'ep', 0, 0, tiled=True)  278 us
    all_to_all x1, waiting for transfers between devices, local_step(): lax.all_to_all(hid_buf.reshape(n_ep, local_exp, slot_cap, d_model), 'ep',...  195 us
    all_to_all x1, waiting for transfers between devices, local_step(): lax.all_to_all(grad_buf.reshape(n_ep, local_exp, slot_cap, d_model), 'ep'...  184 us
    unnamed x112, local copies, waits for them, and re-layouts  97.8 us
  transfers between devices with their start and end apart: 5, of which 4 were waited for; matrix products, arithmetic and copies ran while one was open for 11% of the time, Pallas kernels for 0%

commit v1 on v0

v1 whole, which is shorter than its diff:
```python
import functools

import jax
import jax.numpy as jnp
from jax import lax
from jax.experimental import pallas as pl
from jax.experimental.pallas import tpu as pltpu
from jax.sharding import PartitionSpec as P


LN_EPS = 1e-5
F32 = jnp.float32
BF16 = jnp.bfloat16
VMEM_LIMIT = 63 * 1024 * 1024
D_TILE = 1024
ROW_TILE = 128
COL_TILE = 512
NEG = -1e30


NN = (((1,), (0,)), ((), ()))
NT = (((1,), (1,)), ((), ()))
TN = (((0,), (0,)), ((), ()))

POS_ONE, POS_TWO, GATE_ONE, GATE_TWO, REL_ONE, REL_TWO, MEAN, INV_STD = range(8)

ANY = pl.BlockSpec(memory_space=pl.ANY)
SMEM = pl.BlockSpec(memory_space=pltpu.SMEM)


def mm(left, right, dims=NN):
    return lax.dot_general(left, right, dims, preferred_element_type=F32)


def params(n_axes):
    return pltpu.CompilerParams(dimension_semantics=("arbitrary",) * n_axes, vmem_limit_bytes=VMEM_LIMIT)


def cost(flops, n_bytes, transcendentals=0):
    return pl.CostEstimate(flops=int(flops), bytes_accessed=int(n_bytes), transcendentals=int(transcendentals))


def front_body(n_loc, slot_cap, ep_ref, x_ref, norm_ref, router_ref, first_ref, second_ref, elig_ref,
               slot_one_ref, slot_two_ref, h_ref, meta_ref, cols_ref, diff_one_ref, diff_two_ref):
    x_float = x_ref[...].astype(F32)
    mean = jnp.mean(x_float, axis=-1, keepdims=True)
    centered = x_float - mean
    inv_std = lax.rsqrt(jnp.mean(centered * centered, axis=-1, keepdims=True) + LN_EPS)
    hidden = (centered * inv_std * norm_ref[0:1, :] + norm_ref[1:2, :]).astype(BF16)
    h_ref[...] = hidden
    n_row = x_float.shape[0]
    n_exp = elig_ref.shape[0]
    logits = jnp.concatenate([mm(hidden, router_ref[...], NT), jnp.zeros((n_row, n_row - n_exp), F32)], axis=1).T[:n_exp]
    ids = lax.broadcasted_iota(jnp.int32, (n_exp, n_row), 0)
    first, second = first_ref[...], second_ref[...]
    pick_one = ids == first
    pick_two = ids == second
    allowed = elig_ref[...] > 0
    tabs = []
    for mask, pick in ((allowed, pick_one), (allowed & jnp.logical_not(pick_one), pick_two)):
        masked = jnp.where(mask, logits, NEG)
        powers = jnp.exp(masked - jnp.max(masked, axis=0, keepdims=True))
        prob = powers / jnp.sum(powers, axis=0, keepdims=True)
        hot = jnp.where(pick, 1.0, 0.0)
        tabs.append((jnp.sum(prob * hot, axis=0, keepdims=True), hot - prob))
    rows = []
    for expert, slot in ((first, slot_one_ref[...]), (second, slot_two_ref[...])):
        rows.append(jnp.where(slot >= 0, expert * slot_cap + slot, -1).astype(F32))
    rows += [tabs[0][0], tabs[1][0]]
    for expert, slot in ((first, slot_one_ref[...]), (second, slot_two_ref[...])):
        block = expert ^ (ep_ref[0] * n_loc)
        rows.append(jnp.where(slot >= 0, block * slot_cap + slot, -1).astype(F32))
    rows += [jnp.zeros_like(rows[0])] * 2
    meta = jnp.concatenate(rows, axis=0)
    meta_ref[...] = meta
    fill = jnp.zeros((n_row - n_exp, n_row), F32)
    lanes = lax.broadcasted_iota(jnp.int32, (n_row, n_row), 1)
    cols = jnp.concatenate([meta, fill], axis=0).T
    cols_ref[...] = jnp.where(lanes == MEAN, mean, jnp.where(lanes == INV_STD, inv_std, cols))
    diff_one_ref[...] = jnp.concatenate([tabs[0][1], fill], axis=0).T
    diff_two_ref[...] = jnp.concatenate([tabs[1][1], fill], axis=0).T


def front(ep, tok_x, norm, router_rows, first, second, elig, slot_one, slot_two, n_loc, slot_cap):
    n_tok, d_model = tok_x.shape
    n_exp = elig.shape[0]
    row = pl.BlockSpec((ROW_TILE, d_model), lambda i: (i, 0))
    tab = lambda n: pl.BlockSpec((n, ROW_TILE), lambda i: (0, i))
    col = pl.BlockSpec((ROW_TILE, 128), lambda i: (i, 0))
    wide = jax.ShapeDtypeStruct((n_tok, 128), F32)
    return pl.pallas_call(
        functools.partial(front_body, n_loc, slot_cap),
        grid=(n_tok // ROW_TILE,),
        in_specs=[SMEM, row, pl.BlockSpec(norm.shape, lambda i: (0, 0)), pl.BlockSpec(router_rows.shape, lambda i: (0, 0)),
                  tab(1), tab(1), tab(n_exp), tab(1), tab(1)],
        out_specs=[row, tab(8), col, col, col],
        out_shape=[jax.ShapeDtypeStruct((n_tok, d_model), BF16), jax.ShapeDtypeStruct((8, n_tok), F32), wide, wide, wide],
        compiler_params=params(1), name="front", cost_estimate=cost(2 * n_tok * d_model * 128, 4 * n_tok * d_model),
    )(ep, tok_x, norm, router_rows, first[None], second[None], elig, slot_one[None],
      slot_two[None])


def pick_slots(meta_ref, expert, slot_cap):
    first_row = (expert * slot_cap).astype(F32)
    off_one = meta_ref[POS_ONE:POS_ONE + 1, :] - first_row
    off_two = meta_ref[POS_TWO:POS_TWO + 1, :] - first_row
    in_one = (off_one >= 0) & (off_one < slot_cap)
    in_two = (off_two >= 0) & (off_two < slot_cap)
    slot = jnp.where(in_one, off_one, jnp.where(in_two, off_two, -1.0))
    gate = jnp.where(in_one, meta_ref[GATE_ONE:GATE_ONE + 1, :],
                     jnp.where(in_two, meta_ref[GATE_TWO:GATE_TWO + 1, :], 0.0))
    return slot.astype(jnp.int32), gate


def build_sel(metas, expert, sel_ref, g_ref=None):
    cap, n_tok = sel_ref.shape[1:]
    slot_ids = lax.broadcasted_iota(jnp.int32, (cap, n_tok), 0)
    for src, meta_ref in enumerate(metas):
        slot, gate = pick_slots(meta_ref, expert, cap)
        hit = slot == slot_ids
        sel_ref[src] = jnp.where(hit, 1.0, 0.0).astype(BF16)
        if g_ref is not None:
            g_ref[src * cap:(src + 1) * cap, :] = jnp.sum(jnp.where(hit, gate, 0.0), axis=1, keepdims=True)


def fwd_body(n_k, n_loc, need_o, n_skip, ep_ref, meta_a, meta_b, tok_a, tok_b, wg_ref, wu_ref, *refs):
    refs = list(refs)
    wd_ref = refs.pop(0) if need_o else None
    refs = refs[n_skip:]
    hb_ref, ut_ref, pt_ref, qt_ref = refs[:4]
    o_refs = refs[4:6] if need_o else ()
    sel_ref = refs[-1]
    cap = sel_ref.shape[1]
    k = pl.program_id(1)

    @pl.when(k == 0)
    def _():
        build_sel((meta_a, meta_b), ep_ref[0] * n_loc + pl.program_id(0), sel_ref)

    def gather():
        for src, tok in enumerate((tok_a, tok_b)):
            hb_ref[src * cap:(src + 1) * cap, :] = mm(sel_ref[src], tok[...]).astype(BF16)

    @pl.when(k < n_k - 1)
    def _():
        gather()
        fresh = k == 0
        pt_ref[...] = jnp.where(fresh, 0.0, pt_ref[...]) + mm(wg_ref[...], hb_ref[...], NT)
        qt_ref[...] = jnp.where(fresh, 0.0, qt_ref[...]) + mm(wu_ref[...], hb_ref[...], NT)

    @pl.when(k == n_k - 1)
    def _():
        gather()
        rows = pt_ref.shape[1]
        for c in range(0, rows, 256):
            part = slice(c, c + 256)
            pre_gate = pt_ref[:, part] + mm(wg_ref[...], hb_ref[part, :], NT)
            pre_up = qt_ref[:, part] + mm(wu_ref[...], hb_ref[part, :], NT)
            sig = jax.nn.sigmoid(pre_gate)
            silu = pre_gate * sig
            ut_ref[:, part] = (silu * pre_up).astype(BF16)
            pt_ref[:, part] = pre_up * (sig * (1.0 + pre_gate * (1.0 - sig)))
            qt_ref[:, part] = silu

    if need_o:
        @pl.when(k >= n_k)
        def _():
            out = mm(ut_ref[...], wd_ref[...], TN).astype(BF16)
            o_refs[0][...] = out[:cap]
            o_refs[1][...] = out[cap:]


def bwd_body(n_k, n_loc, need_dh, n_skip, ep_ref, meta_a, meta_b, tok_a, tok_b, wd_ref, pt_hbm, qt_hbm, *refs):
    refs = list(refs)
    if need_dh:
        wg_ref, wu_ref = refs.pop(0), refs.pop(0)
    refs = refs[n_skip:]
    qb_ref, dat_ref, dbt_ref = refs[:3]
    dh_refs = refs[3:5] if need_dh else ()
    sel_ref, g_ref, acc_ref, pt_ref, qt_ref, sems = refs[-6:]
    cap = sel_ref.shape[1]
    j = pl.program_id(0)
    k = pl.program_id(1)
    copies = (pltpu.make_async_copy(pt_hbm.at[j], pt_ref, sems.at[0]),
              pltpu.make_async_copy(qt_hbm.at[j], qt_ref, sems.at[1]))

    @pl.when(k == 0)
    def _():
        for copy in copies:
            copy.start()
        build_sel((meta_a, meta_b), ep_ref[0] * n_loc + j, sel_ref, g_ref)

    def gather():
        for src, tok in enumerate((tok_a, tok_b)):
            rows = slice(src * cap, (src + 1) * cap)
            qb_ref[rows, :] = (g_ref[rows, :] * mm(sel_ref[src], tok[...])).astype(BF16)

    @pl.when(k < n_k - 1)
    def _():
        gather()
        acc_ref[...] = jnp.where(k == 0, 0.0, acc_ref[...]) + mm(wd_ref[...], qb_ref[...], NT)

    @pl.when(k == n_k - 1)
    def _():
        for copy in copies:
            copy.wait()
        gather()
        for c in range(0, acc_ref.shape[1], 256):
            part = slice(c, c + 256)
            grad_inner = acc_ref[:, part] + mm(wd_ref[...], qb_ref[part, :], NT)
            dat_ref[:, part] = (grad_inner * pt_ref[:, part]).astype(BF16)
            dbt_ref[:, part] = (grad_inner * qt_ref[:, part]).astype(BF16)

    if need_dh:
        @pl.when(k >= n_k)
        def _():
            out = (mm(dat_ref[...], wg_ref[...], TN) + mm(dbt_ref[...], wu_ref[...], TN)).astype(BF16)
            dh_refs[0][...] = out[:cap]
            dh_refs[1][...] = out[cap:]


def expert_specs(wg, slot_cap, n_tok):
    ff, d_model = wg.shape[1:]
    n_k = d_model // D_TILE
    first = lambda k: jnp.minimum(k, n_k - 1)
    second = lambda k: jnp.maximum(k - n_k, 0)
    meta = pl.BlockSpec((8, n_tok), lambda j, k: (0, 0))
    tok = pl.BlockSpec((n_tok, D_TILE), lambda j, k: (0, first(k)))
    w_in = pl.BlockSpec((None, ff, D_TILE), lambda j, k: (j, 0, first(k)))
    w_out = pl.BlockSpec((None, ff, D_TILE), lambda j, k: (j, 0, second(k)))
    back = pl.BlockSpec((None, slot_cap, D_TILE), lambda j, k: (j, 0, second(k)))
    return n_k, first, meta, tok, w_in, w_out, back


def expert_fwd(ep, metas, toks, wg, wu, wd, slot_cap, group, prev, need_o, deps):
    n_loc, ff, d_model = wg.shape
    n_tok = toks[0].shape[0]
    rows = 2 * slot_cap
    n_k, first, meta, tok, w_in, w_out, back = expert_specs(wg, slot_cap, n_tok)
    in_specs = [SMEM, meta, meta, tok, tok, w_in, w_in]
    args = [ep, *metas, *toks, wg, wu]
    if need_o:
        in_specs.append(w_out)
        args.append(wd)
    aliases = {len(args) + i: i for i in range(len(prev))}
    args += [*prev, *deps]
    in_specs += [ANY] * (len(prev) + len(deps))
    act = pl.BlockSpec((None, ff, rows), lambda j, k: (j, 0, 0))
    out_shape = [jax.ShapeDtypeStruct((n_loc, 2, rows, d_model), BF16),
                 jax.ShapeDtypeStruct((n_loc, ff, 2 * rows), BF16)]
    out_shape += [jax.ShapeDtypeStruct((n_loc, ff, rows), F32)] * 2
    out_specs = [pl.BlockSpec((None, None, rows, D_TILE), lambda j, k: (j, group, 0, first(k))),
                 pl.BlockSpec((None, ff, rows), lambda j, k: (j, 0, group)), act, act]
    if need_o:
        out_shape += [jax.ShapeDtypeStruct((n_loc, slot_cap, d_model), BF16)] * 2
        out_specs += [back] * 2
    flops = 2 * n_loc * rows * d_model * (ff * (3 if need_o else 2) + n_tok)
    return pl.pallas_call(
        functools.partial(fwd_body, n_k, n_loc, need_o, len(prev) + len(deps)),
        grid=(n_loc, n_k * (2 if need_o else 1)),
        in_specs=in_specs, out_specs=out_specs, out_shape=out_shape,
        scratch_shapes=[pltpu.VMEM((2, slot_cap, n_tok), BF16)],
        input_output_aliases=aliases, compiler_params=params(2),
        cost_estimate=cost(flops, 80e6, n_loc * ff * rows),
    )(*args)


def expert_bwd(ep, metas, toks, wg, wu, wd, pt, qt, slot_cap, group, prev, need_dh, deps):
    n_loc, ff, d_model = wg.shape
    n_tok = toks[0].shape[0]
    rows = 2 * slot_cap
    n_k, first, meta, tok, w_in, w_out, back = expert_specs(wg, slot_cap, n_tok)
    in_specs = [SMEM, meta, meta, tok, tok, w_in, ANY, ANY]
    args = [ep, *metas, *toks, wd, pt, qt]
    if need_dh:
        in_specs += [w_out, w_out]
        args += [wg, wu]
    aliases = {len(args) + i: i for i in range(len(prev))}
    args += [*prev, *deps]
    in_specs += [ANY] * (len(prev) + len(deps))
    out_shape = [jax.ShapeDtypeStruct((n_loc, 2, rows, d_model), BF16)]
    out_shape += [jax.ShapeDtypeStruct((n_loc, ff, 2 * rows), BF16)] * 2
    out_specs = [pl.BlockSpec((None, None, rows, D_TILE), lambda j, k: (j, group, 0, first(k)))]
    out_specs += [pl.BlockSpec((None, ff, rows), lambda j, k: (j, 0, group))] * 2
    if need_dh:
        out_shape += [jax.ShapeDtypeStruct((n_loc, slot_cap, d_model), BF16)] * 2
        out_specs += [back] * 2
    flops = 2 * n_loc * rows * d_model * (ff * (3 if need_dh else 1) + n_tok)
    act = pltpu.VMEM((ff, rows), F32)
    return pl.pallas_call(
        functools.partial(bwd_body, n_k, n_loc, need_dh, len(prev) + len(deps)),
        grid=(n_loc, n_k * (2 if need_dh else 1)),
        in_specs=in_specs, out_specs=out_specs, out_shape=out_shape,
        scratch_shapes=[pltpu.VMEM((2, slot_cap, n_tok), BF16), pltpu.VMEM((rows, 1), F32), act, act, act,
                        pltpu.SemaphoreType.DMA((2,))],
        input_output_aliases=aliases, compiler_params=params(2),
        cost_estimate=cost(flops, 80e6),
    )(*args)


def dw_body(n_prev, n_skip, dat_ref, dbt_ref, ut_ref, hb_ref, qb_ref, *refs):
    prev, outs = refs[:n_prev], refs[n_prev + n_skip:]
    hb = hb_ref[...].reshape(-1, hb_ref.shape[-1])
    qb = qb_ref[...].reshape(-1, qb_ref.shape[-1])
    for i, (left, right) in enumerate(((dat_ref, hb), (dbt_ref, hb), (ut_ref, qb))):
        out = mm(left[...], right)
        outs[i][...] = prev[i][...] + out if n_prev else out


def weight_grads(dat, dbt, ut, hb, qb, prev, deps):
    n_loc, ff, n_rows = dat.shape
    rows, d_model = hb.shape[2:]
    tile = 256
    left = pl.BlockSpec((None, ff, n_rows), lambda j, n: (j, 0, 0))
    right = pl.BlockSpec((None, 2, rows, tile), lambda j, n: (j, 0, 0, n))
    out = pl.BlockSpec((None, ff, tile), lambda j, n: (j, 0, n))
    return pl.pallas_call(
        functools.partial(dw_body, len(prev), len(deps)),
        grid=(n_loc, d_model // tile),
        in_specs=[left] * 3 + [right] * 2 + [out] * len(prev) + [ANY] * len(deps),
        out_specs=[out] * 3,
        out_shape=[jax.ShapeDtypeStruct((n_loc, ff, d_model), F32)] * 3,
        input_output_aliases={5 + i: i for i in range(len(prev))},
        compiler_params=params(2), cost_estimate=cost(6 * n_loc * n_rows * ff * d_model, 200e6),
    )(dat, dbt, ut, hb, qb, *prev, *deps)


def fold(values):
    total = values[:, :128]
    for c in range(128, values.shape[1], 128):
        total = total + values[:, c:c + 128]
    return total


def one_hot(cols_ref, which, n_slot):
    n_tok = cols_ref.shape[0]
    ids = lax.broadcasted_iota(jnp.int32, (n_tok, n_slot), 1)
    return ids == cols_ref[:, which:which + 1].astype(jnp.int32)


def mix_body(n_col, n_skip, cols_ref, diff_one_ref, diff_two_ref, x_ref, dy_ref, h_ref, *refs):
    blocks = refs[:4]
    out_ref, s_ref, dr_ref, sel_ref, dot_ref, st_ref = refs[4 + n_skip:]
    i = pl.program_id(0)
    n_tok = x_ref.shape[0]

    @pl.when(i == 0)
    def _():
        for k, which in enumerate((REL_ONE, REL_TWO)):
            sel_ref[k] = jnp.where(one_hot(cols_ref, which, sel_ref.shape[2]), 1.0, 0.0).astype(BF16)
        dot_ref[...] = jnp.zeros_like(dot_ref)

    @pl.when(i < n_col)
    def _():
        parts = [blk[...].reshape(-1, blk.shape[-1]) for blk in blocks]
        n_part = parts[0].shape[0]
        half = n_tok // 2
        for r in range(0, n_tok, half):
            rows = slice(r, r + half)
            dy_float = dy_ref[rows, :].astype(F32)
            mixed = x_ref[rows, :].astype(F32)
            for k, gate in enumerate((GATE_ONE, GATE_TWO)):
                out = mm(sel_ref[k, rows, :n_part], parts[0])
                for b in range(1, 4):
                    out = out + mm(sel_ref[k, rows, b * n_part:(b + 1) * n_part], parts[b])
                dot_ref[k, rows, :] += fold(dy_float * out)
                mixed = mixed + cols_ref[rows, gate:gate + 1] * out
            out_ref[rows, :] = mixed.astype(BF16)

    @pl.when(i == n_col)
    def _():
        total = jnp.zeros(diff_one_ref.shape, F32)
        for k, (gate, diff) in enumerate(((GATE_ONE, diff_one_ref), (GATE_TWO, diff_two_ref))):
            scale = jnp.sum(dot_ref[k], axis=1, keepdims=True) * cols_ref[:, gate:gate + 1]
            total = total + scale * diff[...]
        s_ref[...] = total.astype(BF16)
        st_ref[...] = total.T.astype(BF16)

    @pl.when(i >= n_col)
    def _():
        dr_ref[...] = mm(st_ref[...], h_ref[...])[:dr_ref.shape[0]]


def mix(cols, diff_one, diff_two, tok_x, tok_dy, hidden, blocks, n_exp, deps):
    n_tok, d_model = tok_x.shape
    n_loc, cap, _ = blocks[0].shape
    n_col = d_model // COL_TILE
    h_tile = 2 * COL_TILE
    first = lambda i: jnp.minimum(i, n_col - 1)
    second = lambda i: jnp.maximum(i - n_col, 0)
    whole = pl.BlockSpec((n_tok, 128), lambda i: (0, 0))
    tile = pl.BlockSpec((n_tok, COL_TILE), lambda i: (0, first(i)))
    block = pl.BlockSpec((n_loc, cap, COL_TILE), lambda i: (0, 0, first(i)))
    n_slot = 4 * n_loc * cap
    return pl.pallas_call(
        functools.partial(mix_body, n_col, len(deps)),
        grid=(n_col + d_model // h_tile,),
        in_specs=[whole] * 3 + [tile] * 2 + [pl.BlockSpec((n_tok, h_tile), lambda i: (0, second(i)))] + [block] * 4
        + [ANY] * len(deps),
        out_specs=[tile, whole, pl.BlockSpec((n_exp, h_tile), lambda i: (0, second(i)))],
        out_shape=[jax.ShapeDtypeStruct((n_tok, d_model), BF16), jax.ShapeDtypeStruct((n_tok, 128), BF16),
                   jax.ShapeDtypeStruct((n_exp, d_model), F32)],
        scratch_shapes=[pltpu.VMEM((2, n_tok, n_slot), BF16), pltpu.VMEM((2, n_tok, 128), F32),
                        pltpu.VMEM((128, n_tok), BF16)],
        compiler_params=params(1), name="mix", cost_estimate=cost(4 * n_tok * n_slot * d_model, 60e6),
    )(cols, diff_one, diff_two, tok_x, tok_dy, hidden, *blocks, *deps)


def tail_body(n_col, n_skip, cols_ref, s_ref, x_ref, dy_ref, norm_ref, router_ref, *refs):
    blocks = refs[:4]
    dx_ref, sums_ref, sel_ref, gh_ref, dot_ref = refs[4 + n_skip:]
    i = pl.program_id(0)
    n_tok, tile = x_ref.shape
    d_model = n_col * tile

    @pl.when(i == 0)
    def _():
        hit = one_hot(cols_ref, REL_ONE, sel_ref.shape[1]) | one_hot(cols_ref, REL_TWO, sel_ref.shape[1])
        sel_ref[...] = jnp.where(hit, 1.0, 0.0).astype(BF16)
        dot_ref[...] = jnp.zeros_like(dot_ref)

    half = n_tok // 2

    def x_hat(rows):
        return (x_ref[rows, :].astype(F32) - cols_ref[rows, MEAN:MEAN + 1]) * cols_ref[rows, INV_STD:INV_STD + 1]

    @pl.when(i < n_col)
    def _():
        parts = [blk[...].reshape(-1, blk.shape[-1]) for blk in blocks]
        n_part = parts[0].shape[0]
        d_bias = jnp.zeros((1, tile), F32)
        d_weight = jnp.zeros((1, tile), F32)
        for r in range(0, n_tok, half):
            rows = slice(r, r + half)
            grad_h = mm(s_ref[rows, :router_ref.shape[0]], router_ref[...])
            for b in range(4):
                grad_h = grad_h + mm(sel_ref[rows, b * n_part:(b + 1) * n_part], parts[b])
            gh_ref[i, rows, :] = grad_h
            normed = x_hat(rows)
            product = grad_h * normed
            weight = norm_ref[0:1, :]
            dot_ref[0, rows, :] += fold(grad_h * weight)
            dot_ref[1, rows, :] += fold(product * weight)
            d_bias = d_bias + jnp.sum(grad_h, axis=0, keepdims=True)
            d_weight = d_weight + jnp.sum(product, axis=0, keepdims=True)
        sums_ref[0:1, :] = d_weight
        sums_ref[1:2, :] = d_bias

    @pl.when(i == n_col)
    def _():
        for k in range(2):
            total = jnp.sum(dot_ref[k], axis=1, keepdims=True) * (1.0 / d_model)
            dot_ref[k] = jnp.broadcast_to(total, dot_ref.shape[1:])

    @pl.when(i >= n_col)
    def _():
        for r in range(0, n_tok, half):
            rows = slice(r, r + half)
            scaled = gh_ref[i - n_col, rows, :] * norm_ref[0:1, :]
            back = scaled - dot_ref[0, rows, 0:1] - x_hat(rows) * dot_ref[1, rows, 0:1]
            grad = dy_ref[rows, :].astype(F32) + cols_ref[rows, INV_STD:INV_STD + 1] * back
            dx_ref[rows, :] = grad.astype(BF16)


def tail(cols, s_rows, tok_x, tok_dy, norm, router_rows, blocks, deps):
    n_tok, d_model = tok_x.shape
    n_loc, cap, _ = blocks[0].shape
    n_col = d_model // COL_TILE
    first = lambda i: jnp.minimum(i, n_col - 1)
    second = lambda i: jnp.maximum(i - n_col, 0)
    both = lambda i: lax.rem(i, n_col)
    whole = pl.BlockSpec((n_tok, 128), lambda i: (0, 0))
    block = pl.BlockSpec((n_loc, cap, COL_TILE), lambda i: (0, 0, first(i)))
    n_slot = 4 * n_loc * cap
    return pl.pallas_call(
        functools.partial(tail_body, n_col, len(deps)),
        grid=(2 * n_col,),
        in_specs=[whole, whole, pl.BlockSpec((n_tok, COL_TILE), lambda i: (0, both(i))),
                  pl.BlockSpec((n_tok, COL_TILE), lambda i: (0, second(i))),
                  pl.BlockSpec((2, COL_TILE), lambda i: (0, both(i))),
                  pl.BlockSpec((router_rows.shape[0], COL_TILE), lambda i: (0, first(i)))] + [block] * 4 + [ANY] * len(deps),
        out_specs=[pl.BlockSpec((n_tok, COL_TILE), lambda i: (0, second(i))),
                   pl.BlockSpec((2, COL_TILE), lambda i: (0, first(i)))],
        out_shape=[jax.ShapeDtypeStruct((n_tok, d_model), BF16), jax.ShapeDtypeStruct((2, d_model), F32)],
        scratch_shapes=[pltpu.VMEM((n_tok, n_slot), BF16), pltpu.VMEM((n_col, n_tok, COL_TILE), F32),
                        pltpu.VMEM((2, n_tok, 128), F32)],
        compiler_params=params(1), name="tail", cost_estimate=cost(2 * n_tok * n_slot * d_model, 60e6),
    )(cols, s_rows, tok_x, tok_dy, norm, router_rows, *blocks, *deps)


def solution(mesh):
    n_ep = mesh.shape['ep']
    n_dp = mesh.shape['dp']
    n_dev = n_ep * n_dp
    tok_spec = P(('dp', 'ep'), None)
    row_spec = P(('dp', 'ep'))
    exp_spec = P('ep', None, None)
    route = {"sib": 1, "x": 2, "xs": 3, "y": n_ep, "ys": n_ep + 1, "yx": n_ep + 2, "yxs": n_ep + 3}

    def swap(arr, way):
        return lax.ppermute(arr, ('dp', 'ep'), [(i, i ^ route[way]) for i in range(n_dev)])

    def after(arr, done):
        return lax.optimization_barrier((arr, done))[0]

    def step(tok_x, tok_dy, exp_first, exp_second, eligible, slot_first, slot_second,
             ln_weight, ln_bias, router, w_gate, w_up, w_down):
        n_local, _ = tok_x.shape
        n_exp = eligible.shape[1]
        n_loc = w_gate.shape[0]
        slot_cap = 3 * n_local // n_exp
        wg = jnp.swapaxes(w_gate, 1, 2)
        wu = jnp.swapaxes(w_up, 1, 2)
        ep = lax.axis_index('ep').astype(jnp.int32)[None]
        router_rows = router.T
        norm = jnp.stack([ln_weight, ln_bias]).astype(F32)
        hidden, meta, cols, diff_one, diff_two = front(
            ep, tok_x, norm, router_rows, exp_first, exp_second, eligible.T, slot_first, slot_second, n_loc, slot_cap)
        metas = [meta] + [swap(meta, way) for way in route]
        h = {way: swap(hidden, way) for way in ("sib", "x", "y")}
        dy = {way: swap(tok_dy, way) for way in ("sib", "x", "y")}
        for rows in (h, dy):
            rows["xs"] = swap(rows["x"], "sib")
            rows["yx"] = swap(rows["x"], "y")
            rows["ys"] = swap(rows["y"], "sib")
            rows["yxs"] = swap(rows["yx"], "sib")

        def fwd(grp, toks, prev, need_o, deps):
            return expert_fwd(ep, metas[2 * grp:2 * grp + 2], toks, wg, wu, w_down, slot_cap, grp % 2, prev,
                              need_o, deps)

        def bwd(grp, toks, pt, qt, prev, need_dh, deps):
            return expert_bwd(ep, metas[2 * grp:2 * grp + 2], toks, wg, wu, w_down, pt, qt, slot_cap, grp % 2,
                              prev, need_dh, deps)

        hb_a, ut_a, pt0, qt0, o_own, o_sib = fwd(0, (hidden, h["sib"]), (), True, ())
        qb_a, dat_a, dbt_a, dh_own, dh_sib = bwd(0, (tok_dy, dy["sib"]), pt0, qt0, (), True, ())
        hb_a, ut_a, pt1, qt1, o_x, o_xs = fwd(1, (h["x"], h["xs"]), (hb_a, ut_a), True, (dh_own,))
        hb_b, ut_b, pt2, qt2 = fwd(2, (h["y"], h["ys"]), (), False, (pt1,))
        qb_a, dat_a, dbt_a, dh_x, dh_xs = bwd(1, (dy["x"], dy["xs"]), pt1, qt1, (qb_a, dat_a, dbt_a), True,
                                              (pt2,))
        qb_b, dat_b, dbt_b = bwd(2, (dy["y"], dy["ys"]), pt2, qt2, (), False, (qb_a,))
        grads = weight_grads(dat_a, dbt_a, ut_a, hb_a, qb_a, (), (qb_b,))
        blocks = (o_own, swap(o_sib, "sib"), swap(o_x, "x"), swap(o_xs, "xs"))
        out_tok, s_rows, d_router = mix(cols, diff_one, diff_two, tok_x, tok_dy, hidden, blocks, n_exp, (grads[0],))
        hb_b, ut_b, pt3, qt3 = fwd(3, (h["yx"], h["yxs"]), (hb_b, ut_b), False, (s_rows,))
        qb_b, dat_b, dbt_b = bwd(3, (dy["yx"], dy["yxs"]), pt3, qt3, (qb_b, dat_b, dbt_b), False, ())
        dwg, dwu, dwd = weight_grads(dat_b, dbt_b, ut_b, hb_b, qb_b, grads, ())
        blocks = (dh_own, swap(dh_sib, "sib"), swap(dh_x, "x"), swap(dh_xs, "xs"))
        dx_tok, sums = tail(cols, s_rows, tok_x, tok_dy, norm, router_rows, blocks, (dwg,))
        d_router = d_router + after(swap(d_router, "sib"), pt3)
        d_router = d_router + after(swap(d_router, "y"), dat_b)
        d_router = d_router + after(swap(d_router, "x"), sums)
        sums = jnp.sum(lax.all_gather(sums, ('dp', 'ep')), axis=0)
        return (out_tok, dx_tok, jnp.swapaxes(dwg, 1, 2), jnp.swapaxes(dwu, 1, 2), dwd,
                d_router.T, sums[0], sums[1])

    return jax.shard_map(
        step, mesh=mesh,
        in_specs=(tok_spec, tok_spec, row_spec, row_spec, tok_spec, row_spec, row_spec,
                  P(), P(), P(), exp_spec, exp_spec, exp_spec),
        out_specs=(tok_spec, tok_spec, exp_spec, exp_spec, exp_spec, P(), P(), P()),
        check_vma=False)
```

time: 4190 us -> 1270 us (0.30)
  waiting for transfers between devices: 2740 us -> 248 us
  Pallas kernels: 0 us -> 968 us
  matrix products: 667 us -> 0 us
  blocking collectives: 581 us -> 12.7 us
  local copies, waits for them, and re-layouts: 122 us -> 2.12 us
    psum x3 -> x0, waiting for transfers between devices: 2370 us -> none  [the longest x1 1950 us: local_step(): dw_gate = lax.psum(dw_gate, 'dp')]
    pallas_call x0 -> x13, Pallas kernels: none -> 968 us  [the longest x4 317 us: expert_fwd(): pl.pallas_call(functools.partial(fwd_body, n_k, n_loc, need_o, len(prev)...]
    dot_general x18 -> x0, matrix products: 667 us -> none  [the longest x1 64.4 us: local_step(): jnp.einsum('sgcd,gfd->sgcf', grad_recv, w_down, preferred_element_type=f32)]
    all_to_all x2 -> x0, blocking collectives: 557 us -> none  [the longest x1 278 us: local_step(): lax.all_to_all(exp_out, 'ep', 0, 0, tiled=True)]
    all_to_all x2 -> x0, waiting for transfers between devices: 378 us -> none  [the longest x1 195 us: local_step(): lax.all_to_all(hid_buf.reshape(n_ep, local_exp, slot_cap, d_model), 'ep',...]
    ppermute x0 -> x30, waiting for transfers between devices: none -> 248 us  [swap(): lax.ppermute(arr, ('dp', 'ep'), [(i, i ^ route[way]) for i in range(n_dev)])]
    unnamed x112 -> x16, local copies, waits for them, and re-layouts: 97.8 us -> 0.06 us
  transfers between devices with their start and end apart: 5 -> 30, of which waited for: 4 -> 6; matrix products, arithmetic and copies ran while one was open for 11% -> 0% of each run, Pallas kernels for 0% -> 76%
where the time goes in v1:
time: 1270 us; the launch traced here: 1260 us
  Pallas kernels  968 us (76%)
  waiting for transfers between devices  248 us (20%)
  starting transfers between devices  23.4 us (2%)
    pallas_call x4, Pallas kernels, expert_fwd(): pl.pallas_call(functools.partial(fwd_body, n_k, n_loc, need_o, len(prev)...  317 us
    pallas_call x2, Pallas kernels, weight_grads(): pl.pallas_call(functools.partial(dw_body, len(prev), len(deps)), grid=(n_...  259 us
    pallas_call x4, Pallas kernels, expert_bwd(): pl.pallas_call(functools.partial(bwd_body, n_k, n_loc, need_dh, len(prev)...  259 us
    ppermute x30, waiting for transfers between devices, swap(): lax.ppermute(arr, ('dp', 'ep'), [(i, i ^ route[way]) for i in range(n_dev)])  248 us
    pallas_call x1, Pallas kernels, mix(): pl.pallas_call(functools.partial(mix_body, n_col, len(deps)), grid=(n_col...  69.3 us
    pallas_call x1, Pallas kernels, tail(): pl.pallas_call(functools.partial(tail_body, n_col, len(deps)), grid=(2 *...  51.6 us
  transfers between devices with their start and end apart: 30, of which 6 were waited for; matrix products, arithmetic and copies ran while one was open for 0% of the time, Pallas kernels for 76%

profile of v1, /device:TPU:0, one launch (start us, length us, event | category | flops | bytes accessed | tf_op | source)
XLA Modules:
  0.0 1258.6 jit_solution(11678222854510787524)
XLA Ops:
  2.7 12.9 %front.1 = (bf16[1024,4096]{1,0:T(8,128)(2,1)}, f32[8,1024]{1,0:T(8,128)}, f32[1024,128]{1,0:T(8,128)}, f32[1024,128]{1,0:T(8,128)}, f32[1024,128]{1,0:T(8,128)}) custom-call(s32[1]{0:T(128)} %bitcast.ep_ref, bf16[1024,4096]{1,0:T(8,128)(2,1)} %x_ref.5, f32[2,4096]{1,0:T(2,128)} %maximum_convert_fusion.norm_ref, bf16[8,4096]{1,0:T(8,128)(2,1)} %bitcast.16, ...), custom_call_target="tpu_custom_call" | custom-call | flops 1073741824 | bytes 16777216 | tf_op jit(solution)/shard_map/front/pallas_call | solution.py:91
  16.4 2.5 collective-permute-start.5
  20.7 20.9 %collective-permute-done.meta_b = f32[8,1024]{1,0:T(8,128)S(1)} collective-permute-done((f32[8,1024]{1,0:T(8,128)}, f32[8,1024]{1,0:T(8,128)S(1)}, u32[]{:S(2)}, u32[]{:S(2)}) %collective-permute-start) | collective-permute-done | bytes 32800 | tf_op jit(solution)/shard_map/ppermute | solution.py:501
  41.6 2.8 collective-permute-start.3
  44.4 156.1 %collective-permute-done.5.tok_a = bf16[1024,4096]{1,0:T(8,128)(2,1)} collective-permute-done((bf16[1024,4096]{1,0:T(8,128)(2,1)}, bf16[1024,4096]{1,0:T(8,128)(2,1)}, u32[]{:S(2)}, u32[]{:S(2)}) %collective-permute-start.5) | collective-permute-done | bytes 8388640 | tf_op jit(solution)/shard_map/ppermute | solution.py:501
  200.6 93.5 %shard_map.188 = (bf16[2,2,768,4096]{3,2,1,0:T(8,128)(2,1)}, bf16[2,1376,1536]{2,1,0:T(8,128)(2,1)}, f32[2,1376,768]{2,1,0:T(8,128)}, f32[2,1376,768]{2,1,0:T(8,...) custom-call(s32[1]{0:T(128)} %bitcast.ep_ref, f32[8,1024]{1,0:T(8,128)} %get-tuple-element.67.meta_a, ...), custom_call_target="tpu_custom_call" | custom-call | flops 64827162624 | bytes 80000000 | tf_op jit(solution)/shard_map/pallas_call | solution.py:258
  294.1 2.1 collective-permute-start.4
  297.8 87.0 %shard_map.189 = (bf16[2,2,768,4096]{3,2,1,0:T(8,128)(2,1)}, bf16[2,1376,1536]{2,1,0:T(8,128)(2,1)}, bf16[2,1376,1536]{2,1,0:T(8,128)(2,1)}, bf16[2,384,4096]{2,1,0:T(8,128)(2,1)}, bf16[2,384,4096]{2,1,0:T(8,128)(2,1)}) custom-call(s32[1]{0:T(128)} %bitcast.ep_ref, f32[8,1024]{1,0:T(8,128)} %get-tuple-element.67.meta_a, f32[8,1024]{1,0:T(8,128)} %copy-done.7, ...), custom_call_target="tpu_custom_call" | custom-call | flops 64827162624 | bytes 80000000 | tf_op jit(solution)/shard_map/pallas_call | solution.py:290
  387.1 94.0 %shard_map.190 = (bf16[2,2,768,4096]{3,2,1,0:T(8,128)(2,1)}, bf16[2,1376,1536]{2,1,0:T(8,128)(2,1)}, f32[2,1376,768]{2,1,0:T(8,128)}, f32[2,1376,768]{2,1,0:T(8,...) custom-call(s32[1]{0:T(128)} %bitcast.ep_ref, ...), custom_call_target="tpu_custom_call", output_to_operand_aliasing={{0}: (8, {}), {1}: (9, {})} | custom-call | flops 64827162624 | bytes 80000000 | tf_op jit(solution)/shard_map/pallas_call | solution.py:258
  483.4 64.6 %shard_map.191 = (bf16[2,2,768,4096]{3,2,1,0:T(8,128)(2,1)}, bf16[2,1376,1536]{2,1,0:T(8,128)(2,1)}, f32[2,1376,768]{2,1,0:T(8,128)}, f32[2,1376,768]{2,1,0:T(8,128)}) custom-call(s32[1]{0:T(128)} %bitcast.ep_ref, f32[8,1024]{1,0:T(8,128)} %copy-done.3, f32[8,1024]{1,0:T(8,128)} %copy-done.4, bf16[1024,4096]{1,0:T(8,128)(2,1)} %collective-permute-done.14.tok_a, ...), custom_call_target="tpu_custom_call" | custom-call | flops 47513075712 | bytes 80000000 | tf_op jit(solution)/shard_map/pallas_call | solution.py:258
  548.5 87.2 %shard_map.192 = (bf16[2,2,768,4096]{3,2,1,0:T(8,128)(2,1)}, bf16[2,1376,1536]{2,1,0:T(8,128)(2,1)}, bf16[2,1376,1536]{2,1,0:T(8,128)(2,1)}, bf16[2,384,4096]{2,1,0:T(8,128)(2,1)}, bf16[2,384,4096]{2,1,0:T(8,128)(2,1)}) custom-call(s32[1]{0:T(128)} %bitcast.ep_ref, ...), custom_call_target="tpu_custom_call", output_to_operand_aliasing={{0}: (10, {}), {1}: (11, {}), {2}: (12, {})} | custom-call | flops 64827162624 | bytes 80000000 | tf_op jit(solution)/shard_map/pallas_call | solution.py:290
  637.1 27.9 %collective-permute-done.25.tok_a = bf16[1024,4096]{1,0:T(8,128)(2,1)} collective-permute-done((bf16[1024,4096]{1,0:T(8,128)(2,1)}, bf16[1024,4096]{1,0:T(8,128)(2,1)}, u32[]{:S(2)}, u32[]{:S(2)}) %collective-permute-start.25) | collective-permute-done | bytes 8388640 | tf_op jit(solution)/shard_map/ppermute | solution.py:501
  665.0 42.2 %shard_map.193 = (bf16[2,2,768,4096]{3,2,1,0:T(8,128)(2,1)}, bf16[2,1376,1536]{2,1,0:T(8,128)(2,1)}, bf16[2,1376,1536]{2,1,0:T(8,128)(2,1)}) custom-call(s32[1]{0:T(128)} %bitcast.ep_ref, f32[8,1024]{1,0:T(8,128)} %copy-done.3, f32[8,1024]{1,0:T(8,128)} %copy-done.4, bf16[1024,4096]{1,0:T(8,128)(2,1)} %collective-permute-done.16.tok_a, ...), custom_call_target="tpu_custom_call" | custom-call | flops 30198988800 | bytes 80000000 | tf_op jit(solution)/shard_map/pallas_call | solution.py:290
  707.1 123.6 %shard_map.194 = (f32[2,1376,4096]{2,1,0:T(8,128)}, f32[2,1376,4096]{2,1,0:T(8,128)}, f32[2,1376,4096]{2,1,0:T(8,128)}) custom-call(bf16[2,1376,1536]{2,1,0:T(8,128)(2,1)} %get-tuple-element.83.dat_ref, bf16[2,1376,1536]{2,1,0:T(8,128)(2,1)} %get-tuple-element.84.dbt_ref, bf16[2,1376,1536]{2,1,0:T(8,128)(2,1)} %get-tuple-element.85.ut_ref, ...), custom_call_target="tpu_custom_call" | custom-call | flops 103884521472 | bytes 200000000 | tf_op jit(solution)/shard_map/pallas_call | solution.py:317
  831.1 13.7 %collective-permute-done.23.tok_a = bf16[1024,4096]{1,0:T(8,128)(2,1)} collective-permute-done((bf16[1024,4096]{1,0:T(8,128)(2,1)}, bf16[1024,4096]{1,0:T(8,128)(2,1)}, u32[]{:S(2)}, u32[]{:S(2)}) %collective-permute-start.23) | collective-permute-done | bytes 8388640 | tf_op jit(solution)/shard_map/ppermute | solution.py:501
  845.2 69.3 %mix.1 = (bf16[1024,4096]{1,0:T(8,128)(2,1)}, bf16[1024,128]{1,0:T(8,128)(2,1)}, f32[8,4096]{1,0:T(8,128)}) custom-call(f32[1024,128]{1,0:T(8,128)} %get-tuple-element.63.cols_ref, f32[1024,128]{1,0:T(8,128)} %get-tuple-element.64.diff_one_ref, f32[1024,128]{1,0:T(8,128)} %get-tuple-element.65.diff_two_ref, bf16[1024,4096]{1,0:T(8,128)(2,1)} %x_ref.5, ...), custom_call_target="tpu_custom_call" | custom-call | flops 51539607552 | bytes 60000000 | tf_op jit(solution)/shard_map/mix/pallas_call | solution.py:395
  916.7 64.7 %shard_map.195 = (bf16[2,2,768,4096]{3,2,1,0:T(8,128)(2,1)}, bf16[2,1376,1536]{2,1,0:T(8,128)(2,1)}, f32[2,1376,768]{2,1,0:T(8,128)}, f32[2,1376,768]{2,1,0:T(8,128)}) custom-call(s32[1]{0:T(128)} %bitcast.ep_ref, f32[8,1024]{1,0:T(8,128)} %copy-done.5, f32[8,1024]{1,0:T(8,128)} %copy-done.6, ...), custom_call_target="tpu_custom_call", output_to_operand_aliasing={{0}: (7, {}), {1}: (8, {})} | custom-call | flops 47513075712 | bytes 80000000 | tf_op jit(solution)/shard_map/pallas_call | solution.py:258
  982.1 1.6 collective-permute-start.28
  983.7 42.1 %shard_map.196 = (bf16[2,2,768,4096]{3,2,1,0:T(8,128)(2,1)}, bf16[2,1376,1536]{2,1,0:T(8,128)(2,1)}, bf16[2,1376,1536]{2,1,0:T(8,128)(2,1)}) custom-call(s32[1]{0:T(128)} %bitcast.ep_ref, f32[8,1024]{1,0:T(8,128)} %copy-done.5, f32[8,1024]{1,0:T(8,128)} %copy-done.6, ...), custom_call_target="tpu_custom_call", output_to_operand_aliasing={{0}: (8, {}), {1}: (9, {}), {2}: (10, {})} | custom-call | flops 30198988800 | bytes 80000000 | tf_op jit(solution)/shard_map/pallas_call | solution.py:290
  1025.8 135.2 %shard_map.197 = (f32[2,1376,4096]{2,1,0:T(8,128)}, f32[2,1376,4096]{2,1,0:T(8,128)}, f32[2,1376,4096]{2,1,0:T(8,128)}) custom-call(bf16[2,1376,1536]{2,1,0:T(8,128)(2,1)} %get-tuple-element.102.dat_ref, bf16[2,1376,1536]{2,1,0:T(8,128)(2,1)} %get-tuple-element.103.dbt_ref, ...), custom_call_target="tpu_custom_call", output_to_operand_aliasing={{0}: (5, {}), {1}: (6, {}), {2}: (7, {})} | custom-call | flops 103884521472 | bytes 200000000 | tf_op jit(solution)/shard_map/pallas_call | solution.py:317
  1161.1 26.0 %collective-permute-done.20.refs_3_ = bf16[2,384,4096]{2,1,0:T(8,128)(2,1)} collective-permute-done((bf16[2,384,4096]{2,1,0:T(8,128)(2,1)}, bf16[2,384,4096]{2,1,0:T(8,128)(2,1)}, u32[]{:S(2)}, u32[]{:S(2)}) %collective-permute-start.20) | collective-permute-done | bytes 6291488 | tf_op jit(solution)/shard_map/ppermute | solution.py:501
  1187.1 51.6 %tail.1 = (bf16[1024,4096]{1,0:T(8,128)(2,1)}, f32[2,4096]{1,0:T(2,128)}) custom-call(f32[1024,128]{1,0:T(8,128)} %get-tuple-element.63.cols_ref, bf16[1024,128]{1,0:T(8,128)(2,1)} %get-tuple-element.92.refs_2_.s_ref, bf16[1024,4096]{1,0:T(8,128)(2,1)} %x_ref.5, bf16[1024,4096]{1,0:T(8,128)(2,1)} %dy_ref.3, f32[2,4096]{1,0:T(2,128)} %maximum_convert_fusion.norm_ref, ...), custom_call_target="tpu_custom_call" | custom-call | flops 25769803776 | bytes 60000000 | tf_op jit(solution)/shard_map/tail/pallas_call | solution.py:475
  1238.7 12.7 %all-gather.1 = f32[8,2,4096]{2,1,0:T(2,128)S(1)} all-gather(f32[1,2,4096]{2,1,0:T(2,128)} %bitcast.19), channel_id=2, replica_groups=mesh['dp'=2,'ep'=4] {'dp','ep'}, dimensions={0}, use_global_device_ids=true | all-gather | bytes 294912 | tf_op jit(solution)/shard_map/all_gather | solution.py:554
  1253.9 3.6 collective-permute-done.29
  (74 shorter events, 19.5 us)
Async XLA Ops:
  16.4 184.1 %collective-permute-start.5 = (bf16[1024,4096]{1,0:T(8,128)(2,1)}, bf16[1024,4096]{1,0:T(8,128)(2,1)}, u32[]{:S(2)}, u32[]{:S(2)}) collective-permute-start(bf16[1024,4096]{1,0:T(8,128)(2,1)} %get-tuple-element.66.tok_a.h_ref), channel_id=1, source_target_pairs={{0,2},{1,3},{2,0},{3,1},{4,6},{5,7},{6,4},{7,5}} | collective-permute-start | bytes 25165832 | tf_op jit(solution)/shard_map/ppermute | solution.py:501
  19.0 277.3 %collective-permute-start.7 = (bf16[1024,4096]{1,0:T(8,128)(2,1)}, bf16[1024,4096]{1,0:T(8,128)(2,1)}, u32[]{:S(2)}, u32[]{:S(2)}) collective-permute-start(bf16[1024,4096]{1,0:T(8,128)(2,1)} %dy_ref.3), channel_id=1, source_target_pairs={{0,1},{1,0},{2,3},{3,2},{4,5},{5,4},{6,7},{7,6}} | collective-permute-start | bytes 25165832 | tf_op jit(solution)/shard_map/ppermute | solution.py:501
  19.1 278.7 %collective-permute-start.14 = (bf16[1024,4096]{1,0:T(8,128)(2,1)}, bf16[1024,4096]{1,0:T(8,128)(2,1)}, u32[]{:S(2)}, u32[]{:S(2)}) collective-permute-start(bf16[1024,4096]{1,0:T(8,128)(2,1)} %get-tuple-element.66.tok_a.h_ref), channel_id=1, source_target_pairs={{0,4},{1,5},{2,6},{3,7},{4,0},{5,1},{6,2},{7,3}} | collective-permute-start | bytes 25165832 | tf_op jit(solution)/shard_map/ppermute | solution.py:501
  41.6 252.5 %collective-permute-start.3 = (f32[8,1024]{1,0:T(8,128)}, f32[8,1024]{1,0:T(8,128)S(1)}, u32[]{:S(2)}, u32[]{:S(2)}) collective-permute-start(f32[8,1024]{1,0:T(8,128)} %get-tuple-element.67.meta_a), channel_id=1, source_target_pairs={{0,2},{1,3},{2,0},{3,1},{4,6},{5,7},{6,4},{7,5}} | collective-permute-start | bytes 98312 | tf_op jit(solution)/shard_map/ppermute | solution.py:501
  44.4 341.0 %collective-permute-start.10 = (bf16[1024,4096]{1,0:T(8,128)(2,1)}, bf16[1024,4096]{1,0:T(8,128)(2,1)}, u32[]{:S(2)}, u32[]{:S(2)}) collective-permute-start(bf16[1024,4096]{1,0:T(8,128)(2,1)} %dy_ref.3), channel_id=1, source_target_pairs={{0,2},{1,3},{2,0},{3,1},{4,6},{5,7},{6,4},{7,5}} | collective-permute-start | bytes 25165832 | tf_op jit(solution)/shard_map/ppermute | solution.py:501
  200.6 186.2 %collective-permute-start.6 = (bf16[1024,4096]{1,0:T(8,128)(2,1)}, bf16[1024,4096]{1,0:T(8,128)(2,1)}, u32[]{:S(2)}, u32[]{:S(2)}) collective-permute-start(bf16[1024,4096]{1,0:T(8,128)(2,1)} %collective-permute-done.5.tok_a), channel_id=1, source_target_pairs={{0,1},{1,0},{2,3},{3,2},{4,5},{5,4},{6,7},{7,6}} | collective-permute-start | bytes 25165832 | tf_op jit(solution)/shard_map/ppermute | solution.py:501
  294.1 90.7 %collective-permute-start.4 = (f32[8,1024]{1,0:T(8,128)}, f32[8,1024]{1,0:T(8,128)S(1)}, u32[]{:S(2)}, u32[]{:S(2)}) collective-permute-start(f32[8,1024]{1,0:T(8,128)} %get-tuple-element.67.meta_a), channel_id=1, source_target_pairs={{0,3},{1,2},{2,1},{3,0},{4,7},{5,6},{6,5},{7,4}} | collective-permute-start | bytes 98312 | tf_op jit(solution)/shard_map/ppermute | solution.py:501
  296.3 185.5 %collective-permute-start.16 = (bf16[1024,4096]{1,0:T(8,128)(2,1)}, bf16[1024,4096]{1,0:T(8,128)(2,1)}, u32[]{:S(2)}, u32[]{:S(2)}) collective-permute-start(bf16[1024,4096]{1,0:T(8,128)(2,1)} %dy_ref.3), channel_id=1, source_target_pairs={{0,4},{1,5},{2,6},{3,7},{4,0},{5,1},{6,2},{7,3}} | collective-permute-start | bytes 25165832 | tf_op jit(solution)/shard_map/ppermute | solution.py:501
  297.8 185.5 %collective-permute-start.15 = (bf16[1024,4096]{1,0:T(8,128)(2,1)}, bf16[1024,4096]{1,0:T(8,128)(2,1)}, u32[]{:S(2)}, u32[]{:S(2)}) collective-permute-start(bf16[1024,4096]{1,0:T(8,128)(2,1)} %collective-permute-done.14.tok_a), channel_id=1, source_target_pairs={{0,1},{1,0},{2,3},{3,2},{4,5},{5,4},{6,7},{7,6}} | collective-permute-start | bytes 25165832 | tf_op jit(solution)/shard_map/ppermute | solution.py:501
  384.9 96.1 %collective-permute-start.12 = (f32[8,1024]{1,0:T(8,128)}, f32[8,1024]{1,0:T(8,128)S(1)}, u32[]{:S(2)}, u32[]{:S(2)}) collective-permute-start(f32[8,1024]{1,0:T(8,128)} %get-tuple-element.67.meta_a), channel_id=1, source_target_pairs={{0,4},{1,5},{2,6},{3,7},{4,0},{5,1},{6,2},{7,3}} | collective-permute-start | bytes 98312 | tf_op jit(solution)/shard_map/ppermute | solution.py:501
  385.4 95.9 %collective-permute-start.13 = (f32[8,1024]{1,0:T(8,128)}, f32[8,1024]{1,0:T(8,128)S(1)}, u32[]{:S(2)}, u32[]{:S(2)}) collective-permute-start(f32[8,1024]{1,0:T(8,128)} %get-tuple-element.67.meta_a), channel_id=1, source_target_pairs={{0,5},{1,4},{2,7},{3,6},{4,1},{5,0},{6,3},{7,2}} | collective-permute-start | bytes 98312 | tf_op jit(solution)/shard_map/ppermute | solution.py:501
  386.8 161.2 %collective-permute-start.11 = (bf16[1024,4096]{1,0:T(8,128)(2,1)}, bf16[1024,4096]{1,0:T(8,128)(2,1)}, u32[]{:S(2)}, u32[]{:S(2)}) collective-permute-start(bf16[1024,4096]{1,0:T(8,128)(2,1)} %collective-permute-done.10.tok_a), channel_id=1, source_target_pairs={{0,1},{1,0},{2,3},{3,2},{4,5},{5,4},{6,7},{7,6}} | collective-permute-start | bytes 25165832 | tf_op jit(solution)/shard_map/ppermute | solution.py:501
  481.0 349.7 %collective-permute-start.2 = (bf16[2,384,4096]{2,1,0:T(8,128)(2,1)}, bf16[2,384,4096]{2,1,0:T(8,128)(2,1)}, u32[]{:S(2)}, u32[]{:S(2)}) collective-permute-start(bf16[2,384,4096]{2,1,0:T(8,128)(2,1)} %get-tuple-element.69), channel_id=1, source_target_pairs={{0,1},{1,0},{2,3},{3,2},{4,5},{5,4},{6,7},{7,6}} | collective-permute-start | bytes 18874376 | tf_op jit(solution)/shard_map/ppermute | solution.py:501
  481.3 183.6 %collective-permute-start.25 = (bf16[1024,4096]{1,0:T(8,128)(2,1)}, bf16[1024,4096]{1,0:T(8,128)(2,1)}, u32[]{:S(2)}, u32[]{:S(2)}) collective-permute-start(bf16[1024,4096]{1,0:T(8,128)(2,1)} %collective-permute-done.5.tok_a), channel_id=1, source_target_pairs={{0,4},{1,5},{2,6},{3,7},{4,0},{5,1},{6,2},{7,3}} | collective-permute-start | bytes 25165832 | tf_op jit(solution)/shard_map/ppermute | solution.py:501
  481.8 362.9 %collective-permute-start.23 = (bf16[1024,4096]{1,0:T(8,128)(2,1)}, bf16[1024,4096]{1,0:T(8,128)(2,1)}, u32[]{:S(2)}, u32[]{:S(2)}) collective-permute-start(bf16[1024,4096]{1,0:T(8,128)(2,1)} %collective-permute-done.10.tok_a), channel_id=1, source_target_pairs={{0,4},{1,5},{2,6},{3,7},{4,0},{5,1},{6,2},{7,3}} | collective-permute-start | bytes 25165832 | tf_op jit(solution)/shard_map/ppermute | solution.py:501
  483.4 152.4 %collective-permute-start.17 = (bf16[1024,4096]{1,0:T(8,128)(2,1)}, bf16[1024,4096]{1,0:T(8,128)(2,1)}, u32[]{:S(2)}, u32[]{:S(2)}) collective-permute-start(bf16[1024,4096]{1,0:T(8,128)(2,1)} %collective-permute-done.16.tok_a), channel_id=1, source_target_pairs={{0,1},{1,0},{2,3},{3,2},{4,5},{5,4},{6,7},{7,6}} | collective-permute-start | bytes 25165832 | tf_op jit(solution)/shard_map/ppermute | solution.py:501
  548.0 296.7 %collective-permute-start.8 = (bf16[2,384,4096]{2,1,0:T(8,128)(2,1)}, bf16[2,384,4096]{2,1,0:T(8,128)(2,1)}, u32[]{:S(2)}, u32[]{:S(2)}) collective-permute-start(bf16[2,384,4096]{2,1,0:T(8,128)(2,1)} %get-tuple-element.75), channel_id=1, source_target_pairs={{0,2},{1,3},{2,0},{3,1},{4,6},{5,7},{6,4},{7,5}} | collective-permute-start | bytes 18874376 | tf_op jit(solution)/shard_map/ppermute | solution.py:501
  635.8 209.4 %collective-permute-start.9 = (bf16[2,384,4096]{2,1,0:T(8,128)(2,1)}, bf16[2,384,4096]{2,1,0:T(8,128)(2,1)}, u32[]{:S(2)}, u32[]{:S(2)}) collective-permute-start(bf16[2,384,4096]{2,1,0:T(8,128)(2,1)} %get-tuple-element.76), channel_id=1, source_target_pairs={{0,3},{1,2},{2,1},{3,0},{4,7},{5,6},{6,5},{7,4}} | collective-permute-start | bytes 18874376 | tf_op jit(solution)/shard_map/ppermute | solution.py:501
  665.0 251.4 %collective-permute-start.26 = (bf16[1024,4096]{1,0:T(8,128)(2,1)}, bf16[1024,4096]{1,0:T(8,128)(2,1)}, u32[]{:S(2)}, u32[]{:S(2)}) collective-permute-start(bf16[1024,4096]{1,0:T(8,128)(2,1)} %collective-permute-done.25.tok_a), channel_id=1, source_target_pairs={{0,1},{1,0},{2,3},{3,2},{4,5},{5,4},{6,7},{7,6}} | collective-permute-start | bytes 25165832 | tf_op jit(solution)/shard_map/ppermute | solution.py:501
  844.7 316.3 %collective-permute-start.18 = (bf16[2,384,4096]{2,1,0:T(8,128)(2,1)}, bf16[2,384,4096]{2,1,0:T(8,128)(2,1)}, u32[]{:S(2)}, u32[]{:S(2)}) collective-permute-start(bf16[2,384,4096]{2,1,0:T(8,128)(2,1)} %get-tuple-element.93), channel_id=1, source_target_pairs={{0,1},{1,0},{2,3},{3,2},{4,5},{5,4},{6,7},{7,6}} | collective-permute-start | bytes 18874376 | tf_op jit(solution)/shard_map/ppermute | solution.py:501
  845.2 138.5 %collective-permute-start.24 = (bf16[1024,4096]{1,0:T(8,128)(2,1)}, bf16[1024,4096]{1,0:T(8,128)(2,1)}, u32[]{:S(2)}, u32[]{:S(2)}) collective-permute-start(bf16[1024,4096]{1,0:T(8,128)(2,1)} %collective-permute-done.23.tok_a), channel_id=1, source_target_pairs={{0,1},{1,0},{2,3},{3,2},{4,5},{5,4},{6,7},{7,6}} | collective-permute-start | bytes 25165832 | tf_op jit(solution)/shard_map/ppermute | solution.py:501
  914.5 246.5 %collective-permute-start.19 = (bf16[2,384,4096]{2,1,0:T(8,128)(2,1)}, bf16[2,384,4096]{2,1,0:T(8,128)(2,1)}, u32[]{:S(2)}, u32[]{:S(2)}) collective-permute-start(bf16[2,384,4096]{2,1,0:T(8,128)(2,1)} %get-tuple-element.94), channel_id=1, source_target_pairs={{0,2},{1,3},{2,0},{3,1},{4,6},{5,7},{6,4},{7,5}} | collective-permute-start | bytes 18874376 | tf_op jit(solution)/shard_map/ppermute | solution.py:501
  916.1 270.9 %collective-permute-start.20 = (bf16[2,384,4096]{2,1,0:T(8,128)(2,1)}, bf16[2,384,4096]{2,1,0:T(8,128)(2,1)}, u32[]{:S(2)}, u32[]{:S(2)}) collective-permute-start(bf16[2,384,4096]{2,1,0:T(8,128)(2,1)} %get-tuple-element.95), channel_id=1, source_target_pairs={{0,3},{1,2},{2,1},{3,0},{4,7},{5,6},{6,5},{7,4}} | collective-permute-start | bytes 18874376 | tf_op jit(solution)/shard_map/ppermute | solution.py:501
  982.1 269.4 %collective-permute-start.28 = (f32[8,4096]{1,0:T(8,128)}, f32[8,4096]{1,0:T(8,128)}, u32[]{:S(2)}, u32[]{:S(2)}) collective-permute-start(f32[8,4096]{1,0:T(8,128)} %add.9), channel_id=1, source_target_pairs={{0,4},{1,5},{2,6},{3,7},{4,0},{5,1},{6,2},{7,3}} | collective-permute-start | bytes 393224 | tf_op jit(solution)/shard_map/ppermute | solution.py:501
  (14 other events, 598.6 us)
